TPU v7x, 32 devices: a whole 2x2x4 slice. The times are simulated.
32 devices in a mesh: dp: 8 (over z, y), query: 4 (over x, core).
Axes of the slice: x: 2, y: 2, z: 4, core: 2. Of those that a mesh axis runs over, the one named last changes fastest.
Arguments:
- sensors: bfloat16 [3072, 4096], P('dp'), may hold values from -8 to 8
- query_index: int32 [2, 8192], P(None, 'query'), may hold values from 0 to 127
- targets: bfloat16 [3072, 8192], P('dp', 'query'), may hold values from -6 to 6
- w_one: bfloat16 [4096, 1024], P(None, 'query'), may hold values from -0.09375 to 0.09375
- b_one: float32 [1024], P('query'), may hold values from -3 to 3
- w_two: bfloat16 [1024, 512], P('query'), may hold values from -0.1875 to 0.1875
- b_two: float32 [512], replicated, may hold values from -3 to 3
- v_one: float32 [2, 512], replicated, may hold values from -4 to 4
- c_one: float32 [512], replicated, may hold values from -3 to 3
- v_two: bfloat16 [512, 512], replicated, may hold values from -0.25 to 0.25
- c_two: float32 [512], replicated, may hold values from -3 to 3
- v_three: bfloat16 [512, 512], replicated, may hold values from -0.25 to 0.25
- c_three: float32 [512], replicated, may hold values from -3 to 3
Outputs:
- loss: float32 [], replicated
- grad_w_one: float32 [4096, 1024], P('dp', 'query')
- grad_b_one: float32 [1024], P('query')
- grad_w_two: float32 [1024, 512], P('query', 'dp')
- grad_b_two: float32 [512], replicated
- grad_v_one: float32 [2, 512], replicated
- grad_c_one: float32 [512], replicated
- grad_v_two: float32 [512, 512], replicated
- grad_c_two: float32 [512], replicated
- grad_v_three: float32 [512, 512], replicated
- grad_c_three: float32 [512], replicated
All inputs are finite; a program needn't handle non-finite values.
Results may differ from a plain program's by a relative error of at most 0.00075.
Values may be sent and summed in bfloat16 or wider, within the bound.
A program may use at most 128 MiB of HBM per device.

v0:
```python
import math
import jax
import jax.numpy as jnp
from jax import lax
from jax.sharding import PartitionSpec as P

GRID = 128


def contract_rows(left, right, precision=None):
    return lax.dot_general(
        left,
        right,
        (((0,), (0,)), ((), ())),
        precision=precision,
        preferred_element_type=jnp.float32,
    )


def contract_cols(left, right, precision=None):
    return lax.dot_general(
        left,
        right,
        (((1,), (1,)), ((), ())),
        precision=precision,
        preferred_element_type=jnp.float32,
    )


def trunk_forward(coords, v_one, c_one, v_two, c_two, v_three, c_three):
    first_act = jnp.tanh(
        coords[0][:, None] * v_one[0][None, :] + coords[1][:, None] * v_one[1][None, :] + c_one
    )
    first_b = first_act.astype(jnp.bfloat16)
    second_act = jnp.tanh(jnp.dot(first_b, v_two, preferred_element_type=jnp.float32) + c_two)
    second_b = second_act.astype(jnp.bfloat16)
    basis_full = jnp.dot(second_b, v_three, preferred_element_type=jnp.float32) + c_three
    return (first_act, first_b, second_act, second_b, basis_full.astype(jnp.bfloat16))


def trunk_backward(coords, first_act, first_b, second_act, second_b, grad_basis, v_two, v_three):
    grad_basis_b = grad_basis.astype(jnp.bfloat16)
    grad_v_three = contract_rows(second_b, grad_basis_b)
    grad_c_three = jnp.sum(grad_basis, axis=0)
    grad_second = contract_cols(grad_basis_b, v_three) * (1.0 - second_act * second_act)
    grad_second_b = grad_second.astype(jnp.bfloat16)
    grad_v_two = contract_rows(first_b, grad_second_b)
    grad_c_two = jnp.sum(grad_second, axis=0)
    grad_first = contract_cols(grad_second_b, v_two) * (1.0 - first_act * first_act)
    grad_v_one = jnp.dot(
        coords, grad_first, precision=lax.Precision.HIGHEST, preferred_element_type=jnp.float32
    )
    grad_c_one = jnp.sum(grad_first, axis=0)
    return (grad_v_one, grad_c_one, grad_v_two, grad_c_two, grad_v_three, grad_c_three)


def local(
    sensors,
    query_index,
    targets,
    w_one,
    b_one,
    w_two,
    b_two,
    v_one,
    c_one,
    v_two,
    c_two,
    v_three,
    c_three,
):
    dp_count = lax.axis_size("dp")
    func_rows = sensors.shape[0]
    query_rows = query_index.shape[1]
    count_all = func_rows * dp_count * query_rows * lax.axis_size("query")
    grad_scale = 64.0 / math.sqrt(count_all)
    inv_scale = 1.0 / math.sqrt(w_two.shape[1])
    coords_all = query_index.astype(jnp.float32) / (GRID - 1)
    hidden = jnp.tanh(jnp.dot(sensors, w_one, preferred_element_type=jnp.float32) + b_one)
    hidden_b = hidden.astype(jnp.bfloat16)
    partial_value = jnp.dot(hidden_b, w_two, preferred_element_type=jnp.float32)
    coeffs = lax.psum(partial_value, "query") + b_two
    coeffs_b = coeffs.astype(jnp.bfloat16)
    row_share = query_rows // dp_count
    coords_mine = lax.dynamic_slice_in_dim(
        coords_all, lax.axis_index("dp") * row_share, row_share, 1
    )
    first_act, first_b, second_act, second_b, basis_b = trunk_forward(
        coords_mine, v_one, c_one, v_two, c_two, v_three, c_three
    )
    basis_all = lax.all_gather(basis_b, "dp", axis=0, tiled=True)
    prediction = contract_cols(coeffs_b, basis_all) * inv_scale
    misfit = prediction - targets.astype(jnp.float32)
    loss_part = jnp.sum(misfit * misfit)
    misfit_b = (misfit * grad_scale).astype(jnp.bfloat16)
    grad_coeffs = lax.psum(
        jnp.dot(misfit_b, basis_all, preferred_element_type=jnp.float32) * inv_scale, "query"
    )
    grad_coeffs_b = grad_coeffs.astype(jnp.bfloat16)
    loss_value = lax.psum(loss_part, ("dp", "query")) / count_all
    columns = misfit_b
    grad_basis = lax.psum_scatter(
        contract_rows(columns, coeffs_b) * inv_scale, "dp", scatter_dimension=0, tiled=True
    )
    trunk_parts = trunk_backward(
        coords_mine, first_act, first_b, second_act, second_b, grad_basis, v_two, v_three
    )
    grad_w_two_part = contract_rows(hidden_b, grad_coeffs_b)
    grad_pre = contract_cols(grad_coeffs_b, w_two) * (1.0 - hidden * hidden)
    grad_pre_b = grad_pre.astype(jnp.bfloat16)
    grad_b_one, grad_b_two = lax.psum(
        (jnp.sum(grad_pre, axis=0), jnp.sum(grad_coeffs, axis=0)), "dp"
    )
    columns = sensors
    grad_w_one = lax.psum_scatter(
        contract_rows(columns, grad_pre_b), "dp", scatter_dimension=0, tiled=True
    )
    grad_w_two = lax.psum_scatter(grad_w_two_part, "dp", scatter_dimension=1, tiled=True)
    trunk_sums = lax.psum(
        (
            trunk_parts[0],
            trunk_parts[1],
            trunk_parts[2],
            trunk_parts[3],
            trunk_parts[4],
            trunk_parts[5],
        ),
        ("dp", "query"),
    )
    return (
        loss_value,
        grad_w_one,
        grad_b_one,
        grad_w_two,
        grad_b_two,
        trunk_sums[0],
        trunk_sums[1],
        trunk_sums[2],
        trunk_sums[3],
        trunk_sums[4],
        trunk_sums[5],
    )


def solution(mesh):
    placed = (
        P("dp", None),
        P(None, "query"),
        P("dp", "query"),
        P(None, "query"),
        P("query"),
        P("query", None),
        P(),
        P(),
        P(),
        P(),
        P(),
        P(),
        P(),
    )
    return jax.shard_map(
        local,
        mesh=mesh,
        in_specs=placed,
        out_specs=(
            P(),
            P("dp", "query"),
            P("query"),
            P("query", "dp"),
            P(),
            P(),
            P(),
            P(),
            P(),
            P(),
            P(),
        ),
        check_vma=False,
    )
```

profile of v0, /device:TPU:0, one launch (start us, length us, event | category | flops | bytes accessed | tf_op | source)
XLA Modules:
  0.0 356.2 jit_solution(2929589968027508688)
XLA Ops:
  8.1 1.8 copy-done
  9.9 2.6 fusion.2
  12.6 1.1 fusion.19
  14.5 0.8 fusion.24
  15.3 1.4 fusion
  16.7 0.8 copy-done.2
  17.5 2.1 fusion.1
  19.6 32.0 %all-reduce.7.cloned.1.call-done = f32[384,512]{1,0:T(8,128)} async-done(((f32[384,512]{1,0:T(8,128)}), f32[384,512]{1,0:T(8,128)}) %all-reduce.7.cloned.1.call-update) | async-done | bytes 786448 | tf_op jit(solution)/shard_map/psum | solution.py:82
  51.6 19.8 %all-gather.2.cloned.1.call-done = bf16[2048,512]{1,0:T(8,128)(2,1)} async-done(((bf16[256,512]{1,0:T(8,128)(2,1)}), bf16[2048,512]{1,0:T(8,128)(2,1)}) %all-gather.2.cloned.1.call-update) | async-done | bytes 2097168 | tf_op jit(solution)/shard_map/all_gather | solution.py:91
  71.4 4.2 %multiply_reduce_fusion = (f32[]{:T(128)}, f32[384,2048]{1,0:T(8,128)S(1)}) fusion(bf16[384,2048]{1,0:T(8,128)(2,1)} %param.15, bf16[2048,512]{1,0:T(8,128)(2,1)} %all-gather.2.cloned.1.call-done, f32[384,512]{1,0:T(8,128)} %all-reduce.7.cloned.1.call-done, f32[512]{0:T(512)S(1)} %copy-done.7), kind=kOutput, calls=%fused_computation.3 | convolution fusion | flops 809631744 | bytes 7604228 | tf_op jit(solution)/shard_map/dot_general | solution.py:21
  75.6 1.6 copy-done.1
  77.2 1.9 convolution_multiply_fusion.1
  79.2 5.3 %convolution_multiply_fusion = f32[2048,512]{1,0:T(8,128)} fusion(f32[384,2048]{1,0:T(8,128)} %copy-done.1, f32[384,512]{1,0:T(8,128)} %all-reduce.7.cloned.1.call-done, f32[512]{0:T(512)S(1)} %copy-done.7), kind=kOutput, calls=%fused_computation.1 | convolution fusion | flops 808321024 | bytes 8128512 | tf_op jit(solution)/shard_map/dot_general | solution.py:11
  84.6 28.1 %all-reduce.9.cloned.1.call-done = f32[384,512]{1,0:T(8,128)} async-done(((f32[384,512]{1,0:T(8,128)}), f32[384,512]{1,0:T(8,128)}) %all-reduce.9.cloned.1.call-update) | async-done | bytes 786448 | tf_op jit(solution)/shard_map/psum | solution.py:96
  112.8 2.1 fusion.28
  114.8 3.2 convolution_bitcast_fusion
  118.1 2.3 fusion.8
  120.5 51.0 %reduce-scatter.8.cloned.1.call-done = f32[256,512]{1,0:T(8,128)} async-done(((f32[2048,512]{1,0:T(8,128)}), f32[256,512]{1,0:T(8,128)}) %reduce-scatter.8.cloned.1.call-update) | async-done | bytes 524304 | tf_op jit(solution)/shard_map/reduce_scatter | solution.py:102
  171.5 1.8 fusion.27
  173.3 2.2 fusion.4
  175.5 1.3 fusion.13
  176.8 1.2 reduce_sum.56
  178.0 21.5 %all-reduce.2 = (f32[256]{0:T(256)}, f32[512]{0:T(512)}) all-reduce(f32[256]{0:T(256)S(1)} %copy-done.12, f32[512]{0:T(512)S(1)} %reduce_sum.56), channel_id=1, replica_groups=mesh['dp'=8,'query'=4] {'dp'}, use_global_device_ids=true, to_apply=%region_6.0 | all-reduce | flops 768 | bytes 6144 | tf_op jit(solution)/shard_map/psum | solution.py:111
  199.6 1.1 reduce_sum.59
  200.7 1.4 fusion.26
  202.5 38.7 %all-reduce = (f32[]{:T(128)}, f32[2,512]{1,0:T(2,128)}, f32[512]{0:T(512)}, f32[512]{0:T(512)}, f32[512]{0:T(512)}) all-reduce(f32[]{:T(128)} %get-tuple-element.35, f32[2,512]{1,0:T(2,128)S(1)} %fusion.29, f32[512]{0:T(512)S(1)} %get-tuple-element.37, ...), channel_id=1, replica_groups=mesh['dp'=8,'query'=4] {'dp','query'}, use_global_device_ids=true, to_apply=%region_2.0 | all-reduce | flops 2561 | bytes 20488 | tf_op jit(solution)/shard_map/psum | solution.py:100
  241.8 31.0 %reduce-scatter.4.cloned.1.call-done = f32[512,256]{0,1:T(8,128)} async-done(((f32[4096,256]{0,1:T(8,128)}), f32[512,256]{0,1:T(8,128)}) %reduce-scatter.4.cloned.1.call-update) | async-done | bytes 524304 | tf_op jit(solution)/shard_map/reduce_scatter | solution.py:115
  272.8 2.0 copy.24
  274.8 64.7 %reduce-scatter.6.cloned.1.call-done = f32[256,64]{0,1:T(8,128)} async-done(((f32[256,512]{0,1:T(8,128)}), f32[256,64]{0,1:T(8,128)}) %reduce-scatter.6.cloned.1.call-update) | async-done | bytes 65552 | tf_op jit(solution)/shard_map/reduce_scatter | solution.py:118
  339.5 3.7 %all-reduce.11.cloned.1.call-done = (f32[512,512]{1,0:T(8,128)}, f32[512,512]{1,0:T(8,128)}) async-done(((f32[512,512]{1,0:T(8,128)}, f32[512,512]{1,0:T(8,128)}), (f32[512,512]{1,0:T(8,128)}, f32[512,512]{1,0:T(8,128)})) %all-reduce.11.cloned.1.call-update) | async-done | bytes 2097168 | tf_op jit(solution)/shard_map/psum | solution.py:119
  343.2 2.3 copy.29
  345.5 2.3 copy.30
  (42 shorter events, 1.5 us)
Async XLA Ops:
  8.0 1.9 copy-start
  8.0 43.6 %all-reduce.7.cloned.1.call-start = ((), (), s32[]{:S(2)}) async-start(), calls=%async_computation.3 | async-start | bytes 1572864 | tf_op jit(solution)/shard_map/psum | solution.py:82
  9.9 2.6 copy-start.6
  12.5 58.9 %copy-start.7 = (f32[512]{0:T(512)S(1)}, f32[512]{0:T(512)}, u32[]{:S(2)}) copy-start(f32[512]{0:T(512)} %param.19) | copy-start | bytes 6148
  13.7 57.7 %all-gather.2.cloned.1.call-start = ((), (), s32[]{:S(2)}) async-start(), calls=%async_computation.4 | async-start | bytes 2359296 | tf_op jit(solution)/shard_map/all_gather | solution.py:91
  14.5 0.8 copy-start.8
  14.5 2.2 copy-start.10
  16.7 0.8 copy-start.2
  19.6 93.2 %all-reduce.9.cloned.1.call-start = ((), (), s32[]{:S(2)}) async-start(), calls=%async_computation.5 | async-start | bytes 1572864 | tf_op jit(solution)/shard_map/psum | solution.py:96
  71.4 5.8 %copy-start.5 = (bf16[2048,512]{1,0:T(8,128)(2,1)S(1)}, bf16[2048,512]{1,0:T(8,128)(2,1)}, u32[]{:S(2)}) copy-start(bf16[2048,512]{1,0:T(8,128)(2,1)} %all-gather.2.cloned.1.call-done) | copy-start | bytes 6291460
  75.6 1.6 copy-start.1
  79.1 92.3 %reduce-scatter.8.cloned.1.call-start = ((), (), s32[]{:S(2)}) async-start(), calls=%async_computation.8 | async-start | bytes 4718592 | tf_op jit(solution)/shard_map/reduce_scatter | solution.py:102
  84.5 188.2 %reduce-scatter.4.cloned.1.call-start = ((), (), s32[]{:S(2)}) async-start(), calls=%async_computation.6 | async-start | bytes 4718592 | tf_op jit(solution)/shard_map/reduce_scatter | solution.py:115
  118.0 55.2 %copy-start.9 = (f32[1,256]{1,0:T(1,128)S(1)}, f32[1,256]{1,0:T(1,128)}, u32[]{:S(2)}) copy-start(f32[1,256]{1,0:T(1,128)} %copy-done.8) | copy-start | bytes 3076
  118.1 221.4 %reduce-scatter.6.cloned.1.call-start = ((), (), s32[]{:S(2)}) async-start(), calls=%async_computation.7 | async-start | bytes 589824 | tf_op jit(solution)/shard_map/reduce_scatter | solution.py:118
  120.4 222.8 %all-reduce.11.cloned.1.call-start = ((), (), s32[]{:S(2)}) async-start(), calls=%async_computation.9 | async-start | bytes 4194304 | tf_op jit(solution)/shard_map/psum | solution.py:119
  171.5 4.0 %copy-start.3 = (f32[256,512]{1,0:T(8,128)S(1)}, f32[256,512]{1,0:T(8,128)}, u32[]{:S(2)}) copy-start(f32[256,512]{1,0:T(8,128)} %copy-done.2) | copy-start | bytes 1572868
  171.5 4.0 %copy-start.4 = (f32[256,512]{1,0:T(8,128)S(1)}, f32[256,512]{1,0:T(8,128)}, u32[]{:S(2)}) copy-start(f32[256,512]{1,0:T(8,128)} %reduce-scatter.8.cloned.1.call-done) | copy-start | bytes 1572868
  173.3 4.8 %copy-start.12 = (f32[256]{0:T(256)S(1)}, f32[256]{0:T(256)}, u32[]{:S(2)}) copy-start(f32[256]{0:T(256)} %get-tuple-element.41) | copy-start | bytes 3076
  173.3 27.4 %copy-start.11 = (f32[1,256]{1,0:T(1,128)S(1)}, f32[1,256]{1,0:T(1,128)}, u32[]{:S(2)}) copy-start(f32[1,256]{1,0:T(1,128)} %copy-done.10) | copy-start | bytes 3076
  173.3 27.4 %copy-start.13 = (f32[512]{0:T(512)S(1)}, f32[512]{0:T(512)}, u32[]{:S(2)}) copy-start(f32[512]{0:T(512)} %param.21) | copy-start | bytes 6148
Sparse Core Ops, SparseCore 0:
  13.9 37.7 all-reduce.6
  79.2 33.4 all-reduce.8
  176.9 166.2 all-reduce.10
Sparse Core Ops, SparseCore 1:
  19.7 51.7 all-gather.1
  84.6 86.8 reduce-scatter.7
  175.0 97.7 reduce-scatter.3
  276.7 62.7 reduce-scatter.5
where the time goes:
time: 357 us; the launch traced here: 356 us
  waiting for transfers between devices  230 us (64%)
  blocking collectives  60.2 us (17%)
  matrix products  33.3 us (9%)
  between operations  17.4 us (5%)
  local copies, waits for them, and re-layouts  11.7 us (3%)
    reduce_scatter x1, waiting for transfers between devices, local(): lax.psum_scatter(grad_w_two_part, 'dp', scatter_dimension=1, tiled=True)  64.7 us
    reduce_scatter x1, waiting for transfers between devices, local(): lax.psum_scatter(contract_rows(columns, coeffs_b) * inv_scale, 'dp', scat...  51 us
    psum x1, blocking collectives, local(): loss_value = lax.psum(loss_part, ('dp', 'query')) / count_all  38.7 us
    psum x1, waiting for transfers between devices, local(): coeffs = lax.psum(partial_value, 'query') + b_two  32 us
    reduce_scatter x1, waiting for transfers between devices, local(): lax.psum_scatter(contract_rows(columns, grad_pre_b), 'dp', scatter_dimens...  31 us
    psum x1, waiting for transfers between devices, local(): lax.psum(jnp.dot(misfit_b, basis_all, preferred_element_type=jnp.float32)...  28.1 us
    psum x1, blocking collectives, local(): lax.psum((jnp.sum(grad_pre, axis=0), jnp.sum(grad_coeffs, axis=0)), 'dp')  21.5 us
    all_gather x1, waiting for transfers between devices, local(): basis_all = lax.all_gather(basis_b, 'dp', axis=0, tiled=True)  19.8 us
  transfers between devices with their start and end apart: 7, of which 7 were waited for; matrix products, arithmetic and copies ran while one was open for 8% of the time, Pallas kernels for 0%

commit v1 on v0

--- a/solution.py
+++ b/solution.py
@@ -79,7 +79,7 @@
     hidden = jnp.tanh(jnp.dot(sensors, w_one, preferred_element_type=jnp.float32) + b_one)
     hidden_b = hidden.astype(jnp.bfloat16)
     partial_value = jnp.dot(hidden_b, w_two, preferred_element_type=jnp.float32)
-    coeffs = lax.psum(partial_value, "query") + b_two
+    coeffs = jnp.sum(lax.all_gather(partial_value, "query"), axis=0) + b_two
     coeffs_b = coeffs.astype(jnp.bfloat16)
     row_share = query_rows // dp_count
     coords_mine = lax.dynamic_slice_in_dim(

time: 357 us -> 541 us (1.52)
  waiting for transfers between devices: 230 us -> 415 us
    psum x1, waiting for transfers between devices: 3.7 us -> 140 us  [local(): lax.psum((trunk_parts[0], trunk_parts[1], trunk_parts[2], trunk_parts[3],...]
    reduce_scatter x1, waiting for transfers between devices: 51 us -> 84.1 us  [local(): lax.psum_scatter(contract_rows(columns, coeffs_b) * inv_scale, 'dp', scat...]
    psum x1 -> x0, waiting for transfers between devices: 32 us -> none  [local(): coeffs = lax.psum(partial_value, 'query') + b_two]
    all_gather x1, waiting for transfers between devices: 19.8 us -> 48.6 us  [local(): basis_all = lax.all_gather(basis_b, 'dp', axis=0, tiled=True)]
    all_gather x0 -> x1, waiting for transfers between devices: none -> 25.7 us  [local(): coeffs = jnp.sum(lax.all_gather(partial_value, 'query'), axis=0) + b_two]
    reduce_scatter x1, waiting for transfers between devices: 31 us -> 23.5 us  [local(): lax.psum_scatter(contract_rows(columns, grad_pre_b), 'dp', scatter_dimens...]
    unnamed x31 -> x33, local copies, waits for them, and re-layouts: 10.9 us -> 11.4 us
  transfers between devices with their start and end apart: 7 -> 7, of which waited for: 7 -> 7; matrix products, arithmetic and copies ran while one was open for 8% -> 6% of each run, Pallas kernels for 0% -> 0%
where the time goes in v1:
time: 541 us; the launch traced here: 540 us
  waiting for transfers between devices  415 us (77%)
  blocking collectives  58.6 us (11%)
  matrix products  33.3 us (6%)
  between operations  16.1 us (3%)
  local copies, waits for them, and re-layouts  11.4 us (2%)
  other arithmetic  6.22 us (1%)
    psum x1, waiting for transfers between devices, local(): lax.psum((trunk_parts[0], trunk_parts[1], trunk_parts[2], trunk_parts[3],...  140 us
    reduce_scatter x1, waiting for transfers between devices, local(): lax.psum_scatter(contract_rows(columns, coeffs_b) * inv_scale, 'dp', scat...  84.1 us
    reduce_scatter x1, waiting for transfers between devices, local(): lax.psum_scatter(grad_w_two_part, 'dp', scatter_dimension=1, tiled=True)  64 us
    all_gather x1, waiting for transfers between devices, local(): basis_all = lax.all_gather(basis_b, 'dp', axis=0, tiled=True)  48.6 us
    psum x1, blocking collectives, local(): loss_value = lax.psum(loss_part, ('dp', 'query')) / count_all  37.1 us
    psum x1, waiting for transfers between devices, local(): lax.psum(jnp.dot(misfit_b, basis_all, preferred_element_type=jnp.float32)...  28.2 us
    all_gather x1, waiting for transfers between devices, local(): coeffs = jnp.sum(lax.all_gather(partial_value, 'query'), axis=0) + b_two  25.7 us
    reduce_scatter x1, waiting for transfers between devices, local(): lax.psum_scatter(contract_rows(columns, grad_pre_b), 'dp', scatter_dimens...  23.5 us
  transfers between devices with their start and end apart: 7, of which 7 were waited for; matrix products, arithmetic and copies ran while one was open for 6% of the time, Pallas kernels for 0%

profile of v1, /device:TPU:0, one launch (start us, length us, event | category | flops | bytes accessed | tf_op | source)
XLA Modules:
  0.0 540.3 jit_solution(6902809415855481526)
XLA Ops:
  7.2 1.8 copy-done
  9.1 2.6 fusion.2
  11.7 1.1 fusion.19
  14.2 1.4 fusion
  15.7 0.8 copy-done.2
  16.4 2.1 fusion.1
  18.6 25.7 %all-gather.6.cloned.1.call-done = f32[1536,512]{1,0:T(8,128)} async-done(((f32[384,512]{1,0:T(8,128)}), f32[1536,512]{1,0:T(8,128)}) %all-gather.6.cloned.1.call-update) | async-done | bytes 3145744 | tf_op jit(solution)/shard_map/all_gather | solution.py:82
  44.3 3.2 reduce_sum.63
  47.5 48.6 %all-gather.4.cloned.1.call-done = bf16[2048,512]{1,0:T(8,128)(2,1)} async-done(((bf16[256,512]{1,0:T(8,128)(2,1)}), bf16[2048,512]{1,0:T(8,128)(2,1)}) %all-gather.4.cloned.1.call-update) | async-done | bytes 2097168 | tf_op jit(solution)/shard_map/all_gather | solution.py:91
  96.1 4.2 multiply_reduce_fusion
  100.3 1.6 copy-done.1
  101.9 1.9 convolution_multiply_fusion.1
  103.8 5.3 convolution_multiply_fusion
  109.3 28.2 %all-reduce.6.cloned.1.call-done = f32[384,512]{1,0:T(8,128)} async-done(((f32[384,512]{1,0:T(8,128)}), f32[384,512]{1,0:T(8,128)}) %all-reduce.6.cloned.1.call-update) | async-done | bytes 786448 | tf_op jit(solution)/shard_map/psum | solution.py:96
  137.5 2.1 fusion.28
  139.6 3.2 convolution_bitcast_fusion
  142.9 2.3 fusion.8
  145.2 84.1 %reduce-scatter.8.cloned.1.call-done = f32[256,512]{1,0:T(8,128)} async-done(((f32[2048,512]{1,0:T(8,128)}), f32[256,512]{1,0:T(8,128)}) %reduce-scatter.8.cloned.1.call-update) | async-done | bytes 524304 | tf_op jit(solution)/shard_map/reduce_scatter | solution.py:102
  229.3 1.8 fusion.27
  231.1 2.2 fusion.4
  233.3 1.3 fusion.13
  234.6 1.2 reduce_sum.66
  235.9 21.5 %all-reduce.2 = (f32[256]{0:T(256)}, f32[512]{0:T(512)}) all-reduce(f32[256]{0:T(256)S(1)} %copy-done.13, f32[512]{0:T(512)S(1)} %reduce_sum.66), channel_id=1, replica_groups=mesh['dp'=8,'query'=4] {'dp'}, use_global_device_ids=true, to_apply=%region_6.0 | all-reduce | flops 768 | bytes 6144 | tf_op jit(solution)/shard_map/psum | solution.py:111
  257.3 1.1 reduce_sum.69
  258.5 1.4 fusion.26
  260.2 37.1 %all-reduce = (f32[]{:T(128)}, f32[2,512]{1,0:T(2,128)}, f32[512]{0:T(512)}, f32[512]{0:T(512)}, f32[512]{0:T(512)}) all-reduce(f32[]{:T(128)} %get-tuple-element.35, f32[2,512]{1,0:T(2,128)S(1)} %fusion.29, f32[512]{0:T(512)S(1)} %get-tuple-element.37, ...), channel_id=1, replica_groups=mesh['dp'=8,'query'=4] {'dp','query'}, use_global_device_ids=true, to_apply=%region_2.0 | all-reduce | flops 2561 | bytes 20488 | tf_op jit(solution)/shard_map/psum | solution.py:100
  298.0 23.5 %reduce-scatter.4.cloned.1.call-done = f32[512,256]{0,1:T(8,128)} async-done(((f32[4096,256]{0,1:T(8,128)}), f32[512,256]{0,1:T(8,128)}) %reduce-scatter.4.cloned.1.call-update) | async-done | bytes 524304 | tf_op jit(solution)/shard_map/reduce_scatter | solution.py:115
  321.5 2.0 copy.24
  323.6 64.0 %reduce-scatter.6.cloned.1.call-done = f32[256,64]{0,1:T(8,128)} async-done(((f32[256,512]{0,1:T(8,128)}), f32[256,64]{0,1:T(8,128)}) %reduce-scatter.6.cloned.1.call-update) | async-done | bytes 65552 | tf_op jit(solution)/shard_map/reduce_scatter | solution.py:118
  387.5 140.3 %all-reduce.8.cloned.1.call-done = (f32[512,512]{1,0:T(8,128)}, f32[512,512]{1,0:T(8,128)}) async-done(((f32[512,512]{1,0:T(8,128)}, f32[512,512]{1,0:T(8,128)}), (f32[512,512]{1,0:T(8,128)}, f32[512,512]{1,0:T(8,128)})) %all-reduce.8.cloned.1.call-update) | async-done | bytes 2097168 | tf_op jit(solution)/shard_map/psum | solution.py:119
  527.8 2.3 copy.28
  530.1 2.3 copy.29
  (45 shorter events, 2.1 us)
Async XLA Ops:
  7.2 1.9 copy-start
  7.2 6.4 %copy-start.12 = (f32[2,512]{1,0:T(2,128)S(1)}, f32[2,512]{1,0:T(2,128)}, u32[]{:S(2)}) copy-start(f32[2,512]{1,0:T(2,128)} %param.20) | copy-start | bytes 12292
  7.2 37.1 %all-gather.6.cloned.1.call-start = ((), (), s32[]{:S(2)}) async-start(), calls=%async_computation.8 | async-start | bytes 3932160 | tf_op jit(solution)/shard_map/all_gather | solution.py:82
  9.1 2.6 copy-start.6
  12.9 83.2 %all-gather.4.cloned.1.call-start = ((), (), s32[]{:S(2)}) async-start(), calls=%async_computation.3 | async-start | bytes 2359296 | tf_op jit(solution)/shard_map/all_gather | solution.py:91
  13.6 0.6 copy-start.8
  13.6 2.0 copy-start.10
  15.6 0.8 copy-start.2
  16.4 79.7 %copy-start.7 = (f32[512]{0:T(512)S(1)}, f32[512]{0:T(512)}, u32[]{:S(2)}) copy-start(f32[512]{0:T(512)} %param.19) | copy-start | bytes 6148
  18.5 119.0 %all-reduce.6.cloned.1.call-start = ((), (), s32[]{:S(2)}) async-start(), calls=%async_computation.4 | async-start | bytes 1572864 | tf_op jit(solution)/shard_map/psum | solution.py:96
  96.1 5.8 %copy-start.5 = (bf16[2048,512]{1,0:T(8,128)(2,1)S(1)}, bf16[2048,512]{1,0:T(8,128)(2,1)}, u32[]{:S(2)}) copy-start(bf16[2048,512]{1,0:T(8,128)(2,1)} %all-gather.4.cloned.1.call-done) | copy-start | bytes 6291460
  100.3 1.6 copy-start.1
  103.8 125.5 %reduce-scatter.8.cloned.1.call-start = ((), (), s32[]{:S(2)}) async-start(), calls=%async_computation.7 | async-start | bytes 4718592 | tf_op jit(solution)/shard_map/reduce_scatter | solution.py:102
  109.2 212.3 %reduce-scatter.4.cloned.1.call-start = ((), (), s32[]{:S(2)}) async-start(), calls=%async_computation.5 | async-start | bytes 4718592 | tf_op jit(solution)/shard_map/reduce_scatter | solution.py:115
  142.8 88.3 %copy-start.9 = (f32[1,256]{1,0:T(1,128)S(1)}, f32[1,256]{1,0:T(1,128)}, u32[]{:S(2)}) copy-start(f32[1,256]{1,0:T(1,128)} %copy-done.8) | copy-start | bytes 3076
  142.8 244.7 %reduce-scatter.6.cloned.1.call-start = ((), (), s32[]{:S(2)}) async-start(), calls=%async_computation.6 | async-start | bytes 589824 | tf_op jit(solution)/shard_map/reduce_scatter | solution.py:118
  145.2 382.6 %all-reduce.8.cloned.1.call-start = ((), (), s32[]{:S(2)}) async-start(), calls=%async_computation.9 | async-start | bytes 4194304 | tf_op jit(solution)/shard_map/psum | solution.py:119
  229.3 4.0 copy-start.3
  229.3 4.0 copy-start.4
  231.1 4.8 copy-start.13
  231.1 27.4 %copy-start.11 = (f32[1,256]{1,0:T(1,128)S(1)}, f32[1,256]{1,0:T(1,128)}, u32[]{:S(2)}) copy-start(f32[1,256]{1,0:T(1,128)} %copy-done.10) | copy-start | bytes 3076
  231.1 27.3 %copy-start.14 = (f32[512]{0:T(512)S(1)}, f32[512]{0:T(512)}, u32[]{:S(2)}) copy-start(f32[512]{0:T(512)} %param.21) | copy-start | bytes 6148
Sparse Core Ops, SparseCore 0:
  13.0 31.2 all-gather.5
  47.0 49.0 all-gather.3
  103.9 33.5 all-reduce.5
  141.0 88.2 reduce-scatter.7
  232.8 88.7 reduce-scatter.3
  325.3 62.1 reduce-scatter.5
  394.2 133.5 all-reduce.7
